TPU v7x, 32 devices: a whole 2x2x4 slice. The times are simulated.
32 devices in a mesh: row: 4 (over x, core), col: 8 (over z, y).
Axes of the slice: x: 2, y: 2, z: 4, core: 2. Of those that a mesh axis runs over, the one named last changes fastest.
Arguments:
- ancestor_inverse: bfloat16 [24576, 24576], P('row', 'col'), may hold values from -0.0390625 to 0.0390625
- panels: bfloat16 [24576, 3, 512], P(('row', 'col')), may hold values from -1.1953125 to 1.1953125
- diag_inverse: float32 [3, 512, 512], replicated, may hold values from -6 to 6
- tile_mask: int32 [3, 192], replicated, may hold values 0 or 1
Outputs:
- off_diagonal: float32 [24576, 3, 512], P(('row', 'col'))
- diagonal: float32 [3, 512, 512], replicated
All inputs are finite; a program needn't handle non-finite values.
Results may differ from a plain program's by a relative error of at most 0.0003.
Values may be sent and summed in bfloat16 or wider, within the bound.
A program may use at most 192 MiB of HBM per device.

v0:
```python
import jax
import jax.numpy as jnp
from jax import lax
from jax.sharding import PartitionSpec as P


def exchange(partial, axis):
    count = lax.axis_size(axis)
    rows, width = partial.shape
    return lax.psum_scatter(partial, axis, scatter_dimension=0, tiled=True)


def body(ancestor_inverse, panels, diag_inverse, tile_mask):
    row_count = lax.axis_size("row")
    col_count = lax.axis_size("col")
    span = lax.axis_index("row") * col_count + lax.axis_index("col")
    kept_rows = panels.shape[0]
    panel_count = panels.shape[1]
    tile = kept_rows * row_count * col_count // tile_mask.shape[1]
    full_mask = jnp.repeat(tile_mask, tile, axis=1).astype(jnp.bfloat16)
    own_mask = lax.dynamic_slice_in_dim(full_mask, span * kept_rows, kept_rows, 1)
    moves = [
        (index, index % row_count * col_count + index // row_count)
        for index in range(row_count * col_count)
    ]
    masked = [panels[:, p, :] * own_mask[p][:, None] for p in range(panel_count)]
    sent = [lax.ppermute(block, ("row", "col"), moves) for block in masked]
    sides = [lax.all_gather(block, "row", axis=0, tiled=True) for block in sent]
    results, parts = ([], [])
    for p in range(panel_count):
        partial = jnp.dot(ancestor_inverse, sides[p], preferred_element_type=jnp.float32)
        summed = -exchange(partial, "col")
        results.append(summed)
        parts.append(
            lax.dot_general(
                masked[p].astype(jnp.float32),
                summed,
                (((0,), (0,)), ((), ())),
                precision=lax.Precision.HIGHEST,
            )
        )
    off_diagonal = jnp.stack(results, axis=1)
    schur = lax.psum(jnp.stack(parts), ("row", "col"))
    return (off_diagonal, diag_inverse - schur)


def solution(mesh):
    return jax.shard_map(
        body,
        mesh=mesh,
        in_specs=(P("row", "col"), P(("row", "col"), None, None), P(), P()),
        out_specs=(P(("row", "col"), None, None), P()),
        check_vma=False,
    )
```

profile of v0, /device:TPU:0, one launch (start us, length us, event | category | flops | bytes accessed | tf_op | source)
XLA Modules:
  0.0 952.1 jit_solution(13903537531053839367)
XLA Ops:
  7.2 0.0 all-gather.8.cloned.1.call-start
  7.2 0.7 convert_element_type.10
  7.9 0.1 broadcast_bitcast_fusion
  8.1 0.1 copy.9
  8.2 0.1 dynamic-slice_reduce_fusion.2
  8.3 2.0 bitcast_multiply_fusion.2
  10.3 0.0 copy-start.4
  10.3 1.6 collective-permute-start.2
  11.9 0.0 collective-permute-done.2
  11.9 0.0 all-gather.8.cloned.1.call-update
  11.9 0.0 all-gather.4.cloned.1.call-start
  12.0 1.6 collective-permute-start
  13.5 0.0 collective-permute-done
  13.5 0.0 all-gather.4.cloned.1.call-update
  13.6 0.0 all-gather.6.cloned.1.call-start
  13.6 1.5 collective-permute-start.1
  15.1 0.0 all-gather.6.cloned.1.call-update
  15.2 0.0 reduce-scatter.8.cloned.1.call-start
  15.2 86.4 %all-gather.8.cloned.1.call-done = bf16[3072,512]{1,0:T(8,128)(2,1)} async-done(((bf16[768,512]{1,0:T(8,128)(2,1)}), bf16[3072,512]{1,0:T(8,128)(2,1)}) %all-gather.8.cloned.1.call-update) | async-done | bytes 3145744 | tf_op jit(solution)/shard_map/all_gather | solution.py:28
  101.6 27.8 %convolution_bitcast_fusion = f32[6144,512]{0,1:T(8,128)} fusion(bf16[3072,512]{1,0:T(8,128)(2,1)} %all-gather.8.cloned.1.call-done, bf16[6144,3072]{1,0:T(8,128)(2,1)} %param.4), kind=kOutput, calls=%fused_computation | convolution fusion | flops 19327352832 | bytes 53477376 | tf_op jit(solution)/shard_map/dot_general | solution.py:31
  129.4 0.0 reduce-scatter.8.cloned.1.call-update
  129.4 0.2 reduce-scatter.4.cloned.1.call-start
  129.7 5.6 all-gather.4.cloned.1.call-done
  135.3 27.7 %convolution_bitcast_fusion.2 = f32[6144,512]{0,1:T(8,128)} fusion(bf16[3072,512]{1,0:T(8,128)(2,1)} %all-gather.4.cloned.1.call-done, bf16[6144,3072]{1,0:T(8,128)(2,1)} %param.4), kind=kOutput, calls=%fused_computation.2 | convolution fusion | flops 19327352832 | bytes 53477376 | tf_op jit(solution)/shard_map/dot_general | solution.py:31
  163.0 0.0 reduce-scatter.4.cloned.1.call-update
  163.1 0.3 reduce-scatter.6.cloned.1.call-start
  163.3 3.3 all-gather.6.cloned.1.call-done
  166.6 27.7 %convolution_bitcast_fusion.1 = f32[6144,512]{0,1:T(8,128)} fusion(bf16[3072,512]{1,0:T(8,128)(2,1)} %all-gather.6.cloned.1.call-done, bf16[6144,3072]{1,0:T(8,128)(2,1)} %param.4), kind=kOutput, calls=%fused_computation.1 | convolution fusion | flops 19327352832 | bytes 53477376 | tf_op jit(solution)/shard_map/dot_general | solution.py:31
  194.3 0.0 reduce-scatter.6.cloned.1.call-update
  194.3 0.3 all-reduce.2.cloned.1.call-start
  194.6 182.9 %reduce-scatter.8.cloned.1.call-done = f32[768,512]{0,1:T(8,128)} async-done(((f32[6144,512]{0,1:T(8,128)}), f32[768,512]{0,1:T(8,128)}) %reduce-scatter.8.cloned.1.call-update) | async-done | bytes 1572880 | tf_op jit(solution)/shard_map/reduce_scatter | solution.py:10
  377.5 3.1 fusion.12
  380.7 206.9 %reduce-scatter.4.cloned.1.call-done = f32[768,512]{0,1:T(8,128)} async-done(((f32[6144,512]{0,1:T(8,128)}), f32[768,512]{0,1:T(8,128)}) %reduce-scatter.4.cloned.1.call-update) | async-done | bytes 1572880 | tf_op jit(solution)/shard_map/reduce_scatter | solution.py:10
  587.6 3.4 fusion.6
  590.9 206.7 %reduce-scatter.6.cloned.1.call-done = f32[768,512]{0,1:T(8,128)} async-done(((f32[6144,512]{0,1:T(8,128)}), f32[768,512]{0,1:T(8,128)}) %reduce-scatter.6.cloned.1.call-update) | async-done | bytes 1572880 | tf_op jit(solution)/shard_map/reduce_scatter | solution.py:10
  797.6 3.1 fusion.9
  800.7 2.0 pad_maximum_fusion.1
  802.7 0.0 all-reduce.2.cloned.1.call-update
  802.7 1.4 copy-done
  804.1 0.1 negate_bitcast_fusion
  804.2 0.4 copy-done.2
  804.6 0.1 negate_bitcast_fusion.1
  804.7 0.9 copy-done.1
  805.7 0.1 negate_bitcast_fusion.2
  805.8 2.4 pad_maximum_fusion
  808.2 6.2 copy.6
  814.4 126.5 %all-reduce.2.cloned.1.call-done = f32[3,512,512]{2,1,0:T(8,128)} async-done(((f32[3,512,512]{2,1,0:T(8,128)}), f32[3,512,512]{2,1,0:T(8,128)}) %all-reduce.2.cloned.1.call-update) | async-done | bytes 3145744 | tf_op jit(solution)/shard_map/psum | solution.py:43
  941.0 4.3 sub.3
  (7 shorter events, 0.0 us)
Async XLA Ops:
  7.2 94.5 %all-gather.8.cloned.1.call-start = ((), (), s32[]{:S(2)}) async-start(), calls=%async_computation.7 | async-start | bytes 3932160 | tf_op jit(solution)/shard_map/all_gather | solution.py:28
  10.3 119.1 %copy-start.4 = (bf16[768,512]{1,0:T(8,128)(2,1)}, bf16[768,512]{1,0:T(8,128)(2,1)S(1)}, u32[]{:S(2)}) copy-start(bf16[768,512]{1,0:T(8,128)(2,1)S(1)} %get-tuple-element.7) | copy-start | bytes 2359300
  10.3 1.6 collective-permute-start.2
  11.9 123.4 %all-gather.4.cloned.1.call-start = ((), (), s32[]{:S(2)}) async-start(), calls=%async_computation.3 | async-start | bytes 3932160 | tf_op jit(solution)/shard_map/all_gather | solution.py:28
  12.0 1.6 collective-permute-start
  13.6 153.1 %all-gather.6.cloned.1.call-start = ((), (), s32[]{:S(2)}) async-start(), calls=%async_computation.5 | async-start | bytes 3932160 | tf_op jit(solution)/shard_map/all_gather | solution.py:28
  13.6 1.5 collective-permute-start.1
  15.2 362.4 %reduce-scatter.8.cloned.1.call-start = ((), (), s32[]{:S(2)}) async-start(), calls=%async_computation.8 | async-start | bytes 14155776 | tf_op jit(solution)/shard_map/reduce_scatter | solution.py:10
  129.4 458.1 %reduce-scatter.4.cloned.1.call-start = ((), (), s32[]{:S(2)}) async-start(), calls=%async_computation.4 | async-start | bytes 14155776 | tf_op jit(solution)/shard_map/reduce_scatter | solution.py:10
  163.1 634.6 %reduce-scatter.6.cloned.1.call-start = ((), (), s32[]{:S(2)}) async-start(), calls=%async_computation.6 | async-start | bytes 14155776 | tf_op jit(solution)/shard_map/reduce_scatter | solution.py:10
  194.3 746.7 %all-reduce.2.cloned.1.call-start = ((), (), s32[]{:S(2)}) async-start(), calls=%async_computation.9 | async-start | bytes 6291456 | tf_op jit(solution)/shard_map/psum | solution.py:43
  802.7 1.4 copy-start
  802.7 1.9 copy-start.2
  804.1 1.5 copy-start.1
  808.2 132.8 %copy-start.3 = (f32[3,512,512]{2,1,0:T(8,128)S(1)}, f32[3,512,512]{2,1,0:T(8,128)}, u32[]{:S(2)}) copy-start(f32[3,512,512]{2,1,0:T(8,128)} %param.6) | copy-start | bytes 9437188
Sparse Core Ops, SparseCore 0:
  12.0 89.5 all-gather.7
  103.2 32.0 all-gather.3
  136.9 29.7 all-gather.5
  170.0 207.4 reduce-scatter.7
  381.0 206.5 reduce-scatter.3
  591.0 206.5 reduce-scatter.5
  803.7 137.2 all-reduce.1
where the time goes:
time: 953 us; the launch traced here: 952 us
  waiting for transfers between devices  818 us (86%)
  matrix products  92.8 us (10%)
  between operations  14.2 us (1%)
  other arithmetic  11.7 us (1%)
    reduce_scatter x3, waiting for transfers between devices, exchange(): return lax.psum_scatter(partial, axis, scatter_dimension=0, tiled=True)  597 us
    psum x1, waiting for transfers between devices, body(): schur = lax.psum(jnp.stack(parts), ('row', 'col'))  127 us
    all_gather x3, waiting for transfers between devices, body(): sides = [lax.all_gather(block, 'row', axis=0, tiled=True) for block in sent]  95.3 us
    dot_general x3, matrix products, body(): jnp.dot(ancestor_inverse, sides[p], preferred_element_type=jnp.float32)  83.2 us
  transfers between devices with their start and end apart: 10, of which 7 were waited for; matrix products, arithmetic and copies ran while one was open for 10% of the time, Pallas kernels for 0%

commit v1 on v0

--- a/solution.py
+++ b/solution.py
@@ -40,7 +40,7 @@
             )
         )
     off_diagonal = jnp.stack(results, axis=1)
-    schur = lax.psum(jnp.stack(parts), ("row", "col"))
+    schur = lax.psum(lax.psum(jnp.stack(parts), "col"), "row")
     return (off_diagonal, diag_inverse - schur)
 
 

time: 953 us -> 1010 us (1.060)
  waiting for transfers between devices: 818 us -> 879 us
    psum x1 -> x2, waiting for transfers between devices: 127 us -> 187 us  [body(): schur = lax.psum(lax.psum(jnp.stack(parts), 'col'), 'row')]
  transfers between devices with their start and end apart: 10 -> 11, of which waited for: 7 -> 8; matrix products, arithmetic and copies ran while one was open for 10% -> 10% of each run, Pallas kernels for 0% -> 0%
where the time goes in v1:
time: 1010 us
  waiting for transfers between devices  879 us (87%)
  matrix products  92.8 us (9%)
  between operations  14.2 us (1%)
  other arithmetic  11.7 us (1%)
    reduce_scatter x3, waiting for transfers between devices, exchange(): return lax.psum_scatter(partial, axis, scatter_dimension=0, tiled=True)  597 us
    psum x2, waiting for transfers between devices, body(): schur = lax.psum(lax.psum(jnp.stack(parts), 'col'), 'row')  187 us
    all_gather x3, waiting for transfers between devices, body(): sides = [lax.all_gather(block, 'row', axis=0, tiled=True) for block in sent]  95.3 us
    dot_general x3, matrix products, body(): jnp.dot(ancestor_inverse, sides[p], preferred_element_type=jnp.float32)  83.2 us
  transfers between devices with their start and end apart: 11, of which 8 were waited for; matrix products, arithmetic and copies ran while one was open for 10% of the time, Pallas kernels for 0%

profile of v1, /device:TPU:0, one launch (start us, length us, event | category | flops | bytes accessed | tf_op | source)
XLA Modules:
  0.0 1011.8 jit_solution(8316045815498323731)
XLA Ops:
  7.2 0.0 all-gather.8.cloned.1.call-start
  7.2 0.7 convert_element_type.10
  7.9 0.1 broadcast_bitcast_fusion
  8.1 0.1 copy.9
  8.2 0.1 dynamic-slice_reduce_fusion.2
  8.3 2.0 bitcast_multiply_fusion.2
  10.3 0.0 copy-start.4
  10.3 1.6 collective-permute-start.2
  11.9 0.0 all-gather.8.cloned.1.call-update
  11.9 0.0 all-gather.4.cloned.1.call-start
  12.0 1.6 collective-permute-start
  13.5 0.0 all-gather.4.cloned.1.call-update
  13.6 0.0 all-gather.6.cloned.1.call-start
  13.6 1.5 collective-permute-start.1
  15.1 0.0 all-gather.6.cloned.1.call-update
  15.2 0.0 reduce-scatter.8.cloned.1.call-start
  15.2 86.4 %all-gather.8.cloned.1.call-done = bf16[3072,512]{1,0:T(8,128)(2,1)} async-done(((bf16[768,512]{1,0:T(8,128)(2,1)}), bf16[3072,512]{1,0:T(8,128)(2,1)}) %all-gather.8.cloned.1.call-update) | async-done | bytes 3145744 | tf_op jit(solution)/shard_map/all_gather | solution.py:28
  101.6 27.8 %convolution_bitcast_fusion = f32[6144,512]{0,1:T(8,128)} fusion(bf16[3072,512]{1,0:T(8,128)(2,1)} %all-gather.8.cloned.1.call-done, bf16[6144,3072]{1,0:T(8,128)(2,1)} %param.4), kind=kOutput, calls=%fused_computation | convolution fusion | flops 19327352832 | bytes 53477376 | tf_op jit(solution)/shard_map/dot_general | solution.py:31
  129.4 0.0 reduce-scatter.8.cloned.1.call-update
  129.4 0.2 reduce-scatter.4.cloned.1.call-start
  129.7 5.6 all-gather.4.cloned.1.call-done
  135.3 27.7 %convolution_bitcast_fusion.2 = f32[6144,512]{0,1:T(8,128)} fusion(bf16[3072,512]{1,0:T(8,128)(2,1)} %all-gather.4.cloned.1.call-done, bf16[6144,3072]{1,0:T(8,128)(2,1)} %param.4), kind=kOutput, calls=%fused_computation.2 | convolution fusion | flops 19327352832 | bytes 53477376 | tf_op jit(solution)/shard_map/dot_general | solution.py:31
  163.0 0.0 reduce-scatter.4.cloned.1.call-update
  163.1 0.3 reduce-scatter.6.cloned.1.call-start
  163.3 3.3 all-gather.6.cloned.1.call-done
  166.6 27.7 %convolution_bitcast_fusion.1 = f32[6144,512]{0,1:T(8,128)} fusion(bf16[3072,512]{1,0:T(8,128)(2,1)} %all-gather.6.cloned.1.call-done, bf16[6144,3072]{1,0:T(8,128)(2,1)} %param.4), kind=kOutput, calls=%fused_computation.1 | convolution fusion | flops 19327352832 | bytes 53477376 | tf_op jit(solution)/shard_map/dot_general | solution.py:31
  194.3 0.0 reduce-scatter.6.cloned.1.call-update
  194.3 0.3 all-reduce.3.cloned.1.call-start
  194.6 182.9 %reduce-scatter.8.cloned.1.call-done = f32[768,512]{0,1:T(8,128)} async-done(((f32[6144,512]{0,1:T(8,128)}), f32[768,512]{0,1:T(8,128)}) %reduce-scatter.8.cloned.1.call-update) | async-done | bytes 1572880 | tf_op jit(solution)/shard_map/reduce_scatter | solution.py:10
  377.5 3.1 fusion.12
  380.7 206.9 %reduce-scatter.4.cloned.1.call-done = f32[768,512]{0,1:T(8,128)} async-done(((f32[6144,512]{0,1:T(8,128)}), f32[768,512]{0,1:T(8,128)}) %reduce-scatter.4.cloned.1.call-update) | async-done | bytes 1572880 | tf_op jit(solution)/shard_map/reduce_scatter | solution.py:10
  587.6 3.4 fusion.6
  590.9 206.7 %reduce-scatter.6.cloned.1.call-done = f32[768,512]{0,1:T(8,128)} async-done(((f32[6144,512]{0,1:T(8,128)}), f32[768,512]{0,1:T(8,128)}) %reduce-scatter.6.cloned.1.call-update) | async-done | bytes 1572880 | tf_op jit(solution)/shard_map/reduce_scatter | solution.py:10
  797.6 3.1 fusion.9
  800.7 2.0 pad_maximum_fusion.1
  802.7 0.0 all-reduce.3.cloned.1.call-update
  802.7 0.0 all-reduce.5.cloned.1.call-start
  802.8 127.9 %all-reduce.3.cloned.1.call-done = f32[3,512,512]{2,1,0:T(8,128)} async-done(((f32[3,512,512]{2,1,0:T(8,128)}), f32[3,512,512]{2,1,0:T(8,128)}) %all-reduce.3.cloned.1.call-update) | async-done | bytes 3145744 | tf_op jit(solution)/shard_map/psum | solution.py:43
  930.7 0.0 all-reduce.5.cloned.1.call-update
  930.8 0.1 negate_bitcast_fusion
  930.9 1.2 copy-done.2
  932.1 0.1 negate_bitcast_fusion.1
  932.2 0.4 copy-done.1
  932.6 0.1 negate_bitcast_fusion.2
  932.7 2.4 pad_maximum_fusion
  935.2 6.4 copy.6
  941.6 59.0 %all-reduce.5.cloned.1.call-done = f32[3,512,512]{2,1,0:T(8,128)} async-done(((f32[3,512,512]{2,1,0:T(8,128)}), f32[3,512,512]{2,1,0:T(8,128)}) %all-reduce.5.cloned.1.call-update) | async-done | bytes 3145744 | tf_op jit(solution)/shard_map/psum | solution.py:43
  1000.6 4.3 sub.3
  (10 shorter events, 0.0 us)
Async XLA Ops:
  7.2 94.5 %all-gather.8.cloned.1.call-start = ((), (), s32[]{:S(2)}) async-start(), calls=%async_computation.7 | async-start | bytes 3932160 | tf_op jit(solution)/shard_map/all_gather | solution.py:28
  10.3 119.1 %copy-start.4 = (bf16[768,512]{1,0:T(8,128)(2,1)}, bf16[768,512]{1,0:T(8,128)(2,1)S(1)}, u32[]{:S(2)}) copy-start(bf16[768,512]{1,0:T(8,128)(2,1)S(1)} %get-tuple-element.7) | copy-start | bytes 2359300
  10.3 1.6 collective-permute-start.2
  11.9 123.4 %all-gather.4.cloned.1.call-start = ((), (), s32[]{:S(2)}) async-start(), calls=%async_computation.3 | async-start | bytes 3932160 | tf_op jit(solution)/shard_map/all_gather | solution.py:28
  12.0 1.6 collective-permute-start
  13.6 153.1 %all-gather.6.cloned.1.call-start = ((), (), s32[]{:S(2)}) async-start(), calls=%async_computation.5 | async-start | bytes 3932160 | tf_op jit(solution)/shard_map/all_gather | solution.py:28
  13.6 1.5 collective-permute-start.1
  15.2 362.4 %reduce-scatter.8.cloned.1.call-start = ((), (), s32[]{:S(2)}) async-start(), calls=%async_computation.8 | async-start | bytes 14155776 | tf_op jit(solution)/shard_map/reduce_scatter | solution.py:10
  129.4 458.1 %reduce-scatter.4.cloned.1.call-start = ((), (), s32[]{:S(2)}) async-start(), calls=%async_computation.4 | async-start | bytes 14155776 | tf_op jit(solution)/shard_map/reduce_scatter | solution.py:10
  163.1 634.6 %reduce-scatter.6.cloned.1.call-start = ((), (), s32[]{:S(2)}) async-start(), calls=%async_computation.6 | async-start | bytes 14155776 | tf_op jit(solution)/shard_map/reduce_scatter | solution.py:10
  194.3 736.4 %all-reduce.3.cloned.1.call-start = ((), (), s32[]{:S(2)}) async-start(), calls=%async_computation.9 | async-start | bytes 6291456 | tf_op jit(solution)/shard_map/psum | solution.py:43
  802.7 128.0 %copy-start = (f32[768,512]{0,1:T(8,128)S(1)}, f32[768,512]{0,1:T(8,128)}, u32[]{:S(2)}) copy-start(f32[768,512]{0,1:T(8,128)} %reduce-scatter.8.cloned.1.call-done) | copy-start | bytes 4718596
  802.7 197.9 %all-reduce.5.cloned.1.call-start = ((), (), s32[]{:S(2)}) async-start(), calls=%async_computation.10 | async-start | bytes 6291456 | tf_op jit(solution)/shard_map/psum | solution.py:43
  930.7 1.4 copy-start.2
  930.8 1.9 copy-start.1
  935.2 65.4 %copy-start.3 = (f32[3,512,512]{2,1,0:T(8,128)S(1)}, f32[3,512,512]{2,1,0:T(8,128)}, u32[]{:S(2)}) copy-start(f32[3,512,512]{2,1,0:T(8,128)} %param.6) | copy-start | bytes 9437188
Sparse Core Ops, SparseCore 0:
  12.0 89.5 all-gather.7
  103.2 32.0 all-gather.3
  136.9 29.7 all-gather.5
  170.0 207.4 reduce-scatter.7
  381.0 206.5 reduce-scatter.3
  591.0 206.5 reduce-scatter.5
  802.9 127.8 all-reduce.2
  933.1 67.4 all-reduce.4
